TPU v7x, 256 devices: a whole 4x4x8 slice. The times are simulated.
256 devices in a mesh: row: 16 (over y_hi, z), col: 16 (over x, y_lo, core).
Axes of the slice: x: 4, y: 4 (y_hi: 2, y_lo: 2; y = y_hi * 2 + y_lo), z: 8, core: 2. Of those that a mesh axis runs over, the one named last changes fastest.
Arguments:
- interior_factor: float32 [16, 16, 1, 384, 384], P('row', 'col'), as said below
- coupling_in: bfloat16 [16, 16, 1, 384, 2048], P('row', 'col'), may hold values from -1.5 to 1.5
- coupling_back: bfloat16 [16, 16, 1, 384, 2048], P('row', 'col'), may hold values from -1.5 to 1.5
- interface_block: bfloat16 [16, 16, 1, 2048, 2048], P('row', 'col'), may hold values from -6 to 6
- gran_count: int32 [16, 16, 1], replicated, may hold values from 2 to 16, as said below
- gran_index: int32 [16, 16, 1, 16], replicated, may hold values from 0 to 15, as said below
Outputs:
- schur: float32 [16, 3, 1024, 1024], P('row', None, 'col')
Inputs may be any that keep to these rules, and one draw needn't show every extreme that they name: `gran_count`: each entry is an even number of granules; in every row group some subdomain has 16. `gran_index`: each row is an order of the 16 window granules, each once; window granule p of row group r is global granule 8 * r + p modulo 8 * 16; the first gran_count entries are the subdomain's interface granules. `interior_factor`: lower triangular with a positive diagonal.
All inputs are finite; a program needn't handle non-finite values.
Results may differ from a plain program's by a relative error of at most 0.0003.
Values may be sent and summed in bfloat16 or wider, within the bound.
A program may use at most 128 MiB of HBM per device.

v0:
```python
import jax
import jax.numpy as jnp
from jax import lax
from jax.sharding import Mesh
from jax.sharding import PartitionSpec as P

COL = ("col_0", "col_1", "col_2")


def reduced_to_own(blocks, axes, turns):
    inside = blocks.shape[1:]
    blocks = blocks.reshape(*(lax.axis_size(a) for a in axes), *inside)
    blocks = jnp.moveaxis(blocks, turns, range(len(axes))).reshape(-1, *inside)
    for k in turns:
        blocks = lax.psum_scatter(blocks, axes[k], scatter_dimension=0, tiled=True)
    return blocks[0]


def in_blocks(shard, dim, devices):
    before, after = (shard.shape[:dim], shard.shape[dim + 1 :])
    return jnp.moveaxis(shard.reshape(*before, devices, -1, *after), dim, 0)


def summed_rows(shard, axes, turns, dim):
    devices = lax.axis_size(axes)
    return reduced_to_own(in_blocks(shard, dim, devices), axes, turns)


def from_behind(block, axis, distance):
    devices = range(lax.axis_size(axis))
    route = [((i - distance) % len(devices), i) for i in devices]
    return lax.ppermute(block, axis, route)


def select_table(count, index):
    slots = jnp.arange(index.shape[0], dtype=jnp.int32)
    live = (slots < count).astype(jnp.float32)
    return (index[:, None] == slots[None, :]).astype(jnp.float32) * live[:, None]


def place(local, table):
    wing = table.shape[0]
    width = local.shape[0]
    granule = width // wing
    blocks = local.reshape(wing, granule, wing, granule)
    moved = jnp.einsum("ap,aibj,bq->piqj", table, blocks, table, precision=lax.Precision.HIGHEST)
    return moved.reshape(width, width)


def solve_columns(factor, coupling, block_count, block):
    height, width = coupling.shape

    def solve_block(block_no, total):
        piece = lax.dynamic_slice_in_dim(coupling, block_no * block, block, 1).astype(jnp.float32)
        solved = lax.linalg.triangular_solve(factor, piece, left_side=True, lower=True)
        return lax.dynamic_update_slice_in_dim(total, solved, block_no * block, 1)

    solved = lax.fori_loop(0, block_count, solve_block, jnp.zeros((height, width), jnp.float32))
    return solved.astype(jnp.bfloat16)


def schur_rows(solved_in, solved_back, block_count, block):
    width = solved_in.shape[1]

    def product_block(block_no, total):
        columns = lax.dynamic_slice_in_dim(solved_back, block_no * block, block, 1)
        rows_out = lax.dot_general(
            columns, solved_in, (((0,), (0,)), ((), ())), preferred_element_type=jnp.float32
        )
        return lax.dynamic_update_slice_in_dim(total, rows_out, block_no * block, 0)

    return lax.fori_loop(0, block_count, product_block, jnp.zeros((width, width), jnp.float32))


def on_device(interior_factor, coupling_in, coupling_back, interface_block, gran_count, gran_index):
    row_id = lax.axis_index("row")
    col_id = lax.axis_index(COL)
    factors = interior_factor[0, 0]
    inputs = coupling_in[0, 0]
    backs = coupling_back[0, 0]
    own_blocks = interface_block[0, 0]
    width = inputs.shape[-1]
    wing = gran_index.shape[-1]
    granule = width // wing
    block = 2 * granule
    half = width // 2
    my_counts = gran_count[row_id, col_id]
    my_index = gran_index[row_id, col_id]
    my_blocks = my_counts // 2
    member = 0
    solved = [
        (
            solve_columns(factors[member], inputs[member], my_blocks[member], block),
            solve_columns(factors[member], backs[member], my_blocks[member], block),
        )
    ]
    member = 0
    product = schur_rows(solved[member][0], solved[member][1], my_blocks[member], block)
    local = own_blocks[member].astype(jnp.float32) - product
    window = place(local, select_table(my_counts[member], my_index[member]))
    quarters = jnp.stack(
        [window[:half, :half], window[:half, half:], window[half:, :half], window[half:, half:]]
    )
    summed = summed_rows(quarters, COL, (2, 0, 1), 1)
    carried = from_behind(summed[3], "row", 1)
    result = jnp.stack([summed[0] + carried, summed[1], summed[2]])
    return result[None]


def solution(mesh):
    split = Mesh(
        mesh.devices.reshape(mesh.shape["row"], 4, 2, 2), ("row", "col_0", "col_1", "col_2")
    )
    return jax.shard_map(
        on_device,
        mesh=split,
        in_specs=(
            P("row", COL, None, None, None),
            P("row", COL, None, None, None),
            P("row", COL, None, None, None),
            P("row", COL, None, None, None),
            P(),
            P(),
        ),
        out_specs=P("row", None, COL, None),
        check_vma=False,
    )
```

profile of v0, /device:TPU:1, one launch (start us, length us, event | category | flops | bytes accessed | tf_op | source)
XLA Modules:
  0.0 956.2 jit_solution(12714727218626394133)
XLA Ops:
  6.5 1.3 constant_dynamic-slice_fusion.2
  10.4 0.6 compare_convert_fusion
  11.2 38.9 %while.37 = (s32[]{:T(128)}, bf16[384,2048]{1,0:T(8,128)(2,1)S(1)}, s32[]{:T(128)}, bf16[384,2048]{1,0:T(8,128)(2,1)}, f32[384,384]{1,0:T(8,128)}, /*index=5*/s3...) while((s32[]{:T(128)}, bf16[384,2048]{1,0:T(8,128)(2,1)S(1)}, s32[]{:T(128)}, ...), condition=%wide.region_1.3_spmd, body=%wide.region_0.2_spmd.sunk | while | flops 303104000 | bytes 4456816 | solution.py:58
  11.3 1.0 dynamic-slice_convert_fusion.4
  12.2 1.1 fusion.89
  13.4 5.7 while.41
  13.4 0.5 fusion.107
  14.0 1.3 bitcast_dynamic-update-slice_fusion.5
  15.3 0.5 fusion.107
  15.9 1.3 bitcast_dynamic-update-slice_fusion.5
  17.3 0.5 fusion.107
  17.8 1.3 bitcast_dynamic-update-slice_fusion.5
  19.1 29.5 %custom-call.13 = f32[3,128,128]{1,2,0:T(8,128)S(1)} custom-call(f32[3,128,128]{2,1,0:T(8,128)S(1)} %get-tuple-element.316), custom_call_target="InvertDiagBlocksLowerTriangular" | custom-call | tf_op jit(solution)/shard_map/while/body/triangular_solve/custom-call.1 | solution.py:55
  49.8 0.3 fusion.92
  50.1 1.2 copy-done.2
  51.5 39.2 %while.39 = (s32[]{:T(128)}, bf16[384,2048]{1,0:T(8,128)(2,1)S(1)}, s32[]{:T(128)}, bf16[384,2048]{1,0:T(8,128)(2,1)}, f32[384,384]{1,0:T(8,128)}, /*index=5*/s3...) while((s32[]{:T(128)}, bf16[384,2048]{1,0:T(8,128)(2,1)S(1)}, s32[]{:T(128)}, ...), condition=%wide.region_3.5_spmd, body=%wide.region_2.4_spmd.sunk | while | flops 303104000 | bytes 4456816 | solution.py:58
  51.5 1.0 dynamic-slice_convert_fusion.5
  52.5 1.1 fusion.100
  53.6 6.1 while.42
  53.7 0.6 fusion.106
  54.3 1.3 bitcast_dynamic-update-slice_fusion.4
  55.7 0.6 fusion.106
  56.3 1.3 bitcast_dynamic-update-slice_fusion.4
  57.7 0.6 fusion.106
  58.3 1.3 bitcast_dynamic-update-slice_fusion.4
  59.7 29.5 %custom-call.15 = f32[3,128,128]{1,2,0:T(8,128)S(1)} custom-call(f32[3,128,128]{2,1,0:T(8,128)S(1)} %get-tuple-element.323), custom_call_target="InvertDiagBlocksLowerTriangular" | custom-call | tf_op jit(solution)/shard_map/while/body/triangular_solve/custom-call.1 | solution.py:55
  89.8 0.3 fusion.102
  90.4 0.3 fusion.103
  90.7 7.9 broadcast_in_dim.8
  98.6 3.0 while.40
  98.6 3.0 convolution_dynamic-update-slice_fusion.2
  101.6 9.1 fusion.24
  110.7 7.5 copy.21
  118.2 32.3 %fusion.27 = f32[128,16,128,16]{2,3,1,0:T(8,128)} fusion(f32[16,128,16,128]{3,2,1,0:T(8,128)} %bitcast.134, f32[16]{0:T(128)S(1)} %compare_convert_fusion, s32[16]{0:T(128)S(1)} %dynamic-slice_bitcast_fusion), kind=kOutput, calls=%fused_computation.53 | convolution fusion | flops 805306880 | bytes 33554560 | tf_op jit(solution)/shard_map/ap,aibj,bq->piqj/dot_general | solution.py:46
  150.5 27.3 %fusion.29 = f32[16,128,16,128]{3,2,0,1:T(8,128)} fusion(f32[128,16,128,16]{2,3,1,0:T(8,128)} %fusion.27, f32[16]{0:T(128)S(1)} %compare_convert_fusion, s32[16]{0:T(128)S(1)} %dynamic-slice_bitcast_fusion), kind=kOutput, calls=%fused_computation.55 | convolution fusion | flops 805306880 | bytes 33554560 | tf_op jit(solution)/shard_map/ap,aibj,bq->piqj/dot_general | solution.py:46
  177.8 6.8 copy.14
  184.6 6.1 copy.30
  190.7 5.0 fusion.48
  195.7 5.6 pad_maximum_fusion
  201.3 6.1 copy.19
  207.5 602.1 %reduce-scatter.4.cloned.1.call-done = f32[8,4,64,1024]{3,2,1,0:T(8,128)} async-done(((f32[16,4,64,1024]{3,2,1,0:T(8,128)}), f32[8,4,64,1024]{3,2,1,0:T(8,128)}) %reduce-scatter.4.cloned.1.call-update) | async-done | bytes 8388624 | tf_op jit(solution)/shard_map/reduce_scatter | solution.py:15
  809.7 86.3 %reduce-scatter.6.cloned.1.call-done = f32[2,4,64,1024]{3,2,1,0:T(8,128)} async-done(((f32[8,4,64,1024]{3,2,1,0:T(8,128)}), f32[2,4,64,1024]{3,2,1,0:T(8,128)}) %reduce-scatter.6.cloned.1.call-update) | async-done | bytes 2097168 | tf_op jit(solution)/shard_map/reduce_scatter | solution.py:15
  896.0 39.2 %reduce-scatter.8.cloned.1.call-done = f32[1,4,64,1024]{3,2,1,0:T(8,128)} async-done(((f32[2,4,64,1024]{3,2,1,0:T(8,128)}), f32[1,4,64,1024]{3,2,1,0:T(8,128)}) %reduce-scatter.8.cloned.1.call-update) | async-done | bytes 1048592 | tf_op jit(solution)/shard_map/reduce_scatter | solution.py:15
  935.2 1.2 slice_bitcast_fusion.14
  936.4 1.4 collective-permute-start
  937.7 9.6 %collective-permute-done = f32[64,1024]{1,0:T(8,128)S(1)} collective-permute-done((f32[64,1024]{1,0:T(8,128)S(1)}, f32[64,1024]{1,0:T(8,128)S(1)}, u32[]{:S(2)}, u32[]{:S(2)}) %collective-permute-start) | collective-permute-done | bytes 262176 | tf_op jit(solution)/shard_map/ppermute | solution.py:32
  947.3 1.0 fusion.33
  948.3 0.9 maximum_bitcast_fusion
  (35 shorter events, 3.0 us)
Async XLA Ops:
  6.5 3.8 copy-start
  6.5 803.1 %reduce-scatter.4.cloned.1.call-start = ((), (), s32[]{:S(2)}) async-start(), calls=%async_computation.3 | async-start | bytes 25165824 | tf_op jit(solution)/shard_map/reduce_scatter | solution.py:15
  50.1 1.2 copy-start.2
  207.4 741.8 %copy-start.1 = (s32[16,16,1,16]{3,2,1,0:T(1,128)S(1)}, s32[16,16,1,16]{3,2,1,0:T(1,128)}, u32[]{:S(2)}) copy-start(s32[16,16,1,16]{3,2,1,0:T(1,128)} %param.19) | copy-start | bytes 49156
  207.4 688.6 %reduce-scatter.6.cloned.1.call-start = ((), (), s32[]{:S(2)}) async-start(), calls=%async_computation.4 | async-start | bytes 10485760 | tf_op jit(solution)/shard_map/reduce_scatter | solution.py:15
  809.7 125.5 %reduce-scatter.8.cloned.1.call-start = ((), (), s32[]{:S(2)}) async-start(), calls=%async_computation.5 | async-start | bytes 3145728 | tf_op jit(solution)/shard_map/reduce_scatter | solution.py:15
  936.4 11.0 %collective-permute-start = (f32[64,1024]{1,0:T(8,128)S(1)}, f32[64,1024]{1,0:T(8,128)S(1)}, u32[]{:S(2)}, u32[]{:S(2)}) collective-permute-start(f32[64,1024]{1,0:T(8,128)S(1)} %get-tuple-element.163), channel_id=1, source_target_pairs={{240,0},{0,16},{16,32},{32,48},{48,64},{64,80},{80,96},{96,112},{1... | collective-permute-start | bytes 786440 | tf_op jit(solution)/shard_map/ppermute | solution.py:32
Sparse Core Ops, SparseCore 0:
  207.5 602.0 reduce-scatter.3
  812.2 83.7 reduce-scatter.5
  898.5 36.6 reduce-scatter.7
where the time goes:
time: 966 us; the launch traced here: 956 us
  waiting for transfers between devices  737 us (76%)
  other arithmetic  80.5 us (8%)
  matrix products  65.5 us (7%)
  local copies, waits for them, and re-layouts  55 us (6%)
  between operations  16.2 us (2%)
    reduce_scatter x3, waiting for transfers between devices, reduced_to_own(): blocks = lax.psum_scatter(blocks, axes[k], scatter_dimension=0, tiled=True)  728 us
    another operation x8, other arithmetic, solve_block(): lax.linalg.triangular_solve(factor, piece, left_side=True, lower=True)  61.2 us
    dot_general x2, matrix products, place(): jnp.einsum('ap,aibj,bq->piqj', table, blocks, table, precision=lax.Precis...  59.6 us
  transfers between devices with their start and end apart: 4, of which 4 were waited for; matrix products, arithmetic and copies ran while one was open for 0% of the time, Pallas kernels for 0%

commit v1 on v0

v1 whole, which is shorter than its diff:
```python
import functools

import jax
import jax.numpy as jnp
from jax import lax
from jax.experimental import pallas as pl
from jax.experimental.pallas import tpu as pltpu
from jax.sharding import Mesh
from jax.sharding import PartitionSpec as P

MESH = pl.DeviceIdType.MESH
X, Y, CORE = "col_0", "col_1", "col_2"
COL = (X, Y, CORE)
NX = 4
G = 128
HEAD = 16
HIGHEST = lax.Precision.HIGHEST

B_UNITS = ["b1p", "b1m", "b2op", "b2om", "b2sp", "b2sm", "b3"]
A_UNITS = ["a1_2", "a1_1", "a1_3", "a1_0", "a2p", "a2m", "a3op", "a3om", "a3sp", "a3sm"]


def unit_numbers():
    names = []
    for block in (3, 1):
        names += [(block, u) for u in B_UNITS]
    for block in (2, 0):
        names += [(block, u) for u in A_UNITS]
    names.append((3, "carry"))
    return {name: i for i, name in enumerate(names)}


UNIT = unit_numbers()


def mm(a, b):
    return jnp.dot(a, b, precision=HIGHEST, preferred_element_type=jnp.float32)


def inverse_of_block(block):
    n = block.shape[0]
    row = lax.broadcasted_iota(jnp.int32, (n, n), 0)
    col = lax.broadcasted_iota(jnp.int32, (n, n), 1)
    diagonal = jnp.where(row == col, block, 0.0)
    down = 1.0 / jnp.sum(diagonal, axis=1, keepdims=True)
    across = 1.0 / jnp.sum(diagonal, axis=0, keepdims=True)

    def below(size):
        return (
            (row // (2 * size) == col // (2 * size))
            & ((row // size) % 2 == 1)
            & ((col // size) % 2 == 0)
        )

    found = jnp.where(row == col, down, 0.0) - jnp.where(below(1), block, 0.0) * down * across
    size = 2
    while size < n:
        part = jnp.where(below(size), block, 0.0)
        found = found - mm(mm(found, part), found)
        size *= 2
    return found


def kernel(
    tab, live, factor_hbm, in_hbm, back_hbm, own_hbm, out,
    factor, ci, cb, ibo, ibp, w, in_o, in_p, bt, bp, acc, sendb, recvb,
    factor_sem, load_sem, swap_send, swap_recv, send_sem, recv_sem,
):
    row = lax.axis_index("row")
    rows = lax.axis_size("row")
    x = lax.axis_index(X)
    y = lax.axis_index(Y)
    k = lax.axis_index(CORE)
    plus = {X: lax.rem(x + 1, NX)}
    minus = {X: lax.rem(x + NX - 1, NX)}
    over = {Y: 1 - y}
    mate = {CORE: 1 - k}
    after = {"row": lax.rem(row + 1, rows)}
    before = {"row": lax.rem(row + rows - 1, rows)}

    barrier = pltpu.get_barrier_semaphore()
    for to in (mate, plus, minus, over, after, before):
        pl.semaphore_signal(barrier, inc=1, device_id=to, device_id_type=MESH)

    def load_columns(src, dst, q, which):
        return pltpu.make_async_copy(
            src.at[:, pl.ds(q * G, G)], dst.at[q], load_sem.at[which, q]
        )

    loads = [
        [pltpu.make_async_copy(factor_hbm, factor, factor_sem)],
        [load_columns(back_hbm, cb, q, 0) for q in range(16)],
        [load_columns(in_hbm, ci, q, 1) for q in range(16)],
        [
            pltpu.make_async_copy(
                own_hbm.at[:, k, :, pl.ds(q * G, G)], ibo.at[q], load_sem.at[2, q]
            )
            for q in range(16)
        ],
    ]
    for load in loads:
        for copy in load:
            copy.start()

    def wait_for(load):
        for copy in load:
            copy.wait()

    pl.semaphore_wait(barrier, 6)

    def swap(src, dst, n):
        return pltpu.make_async_remote_copy(
            src_ref=src, dst_ref=dst, send_sem=swap_send.at[n], recv_sem=swap_recv.at[n],
            device_id=mate, device_id_type=MESH,
        )

    swaps = {
        "back1": swap(bt.at[pl.ds(8, 8), 1 - k], bp.at[pl.ds(8, 8)], 16),
        "back0": swap(bt.at[pl.ds(0, 8), 1 - k], bp.at[pl.ds(0, 8)], 17),
        "in1": swap(in_o.at[:, pl.ds(1024, 1024)], in_p.at[:, pl.ds(1024, 1024)], 18),
        "in0": swap(in_o.at[:, pl.ds(0, 1024)], in_p.at[:, pl.ds(0, 1024)], 19),
    }
    for q in range(16):
        swaps[q] = swap(own_hbm.at[:, 1 - k, :, pl.ds(q * G, G)], ibp.at[q], q)
        swaps[q].start()

    wait_for(loads[0])
    n = factor.shape[0]

    def part(i, j):
        return factor[i * G : (i + 1) * G, j * G : (j + 1) * G]

    x0, x1, x2 = (inverse_of_block(part(i, i)) for i in range(3))
    x10 = -mm(mm(x1, part(1, 0)), x0)
    t0 = mm(x2, part(2, 0))
    t1 = mm(x2, part(2, 1))
    x20 = -(mm(t0, x0) + mm(t1, x10))
    x21 = -mm(t1, x1)
    zero = jnp.zeros((G, G), jnp.float32)
    for i, line in enumerate(((x0, zero, zero), (x10, x1, zero), (x20, x21, x2))):
        for j, piece in enumerate(line):
            high = piece.astype(jnp.bfloat16)
            w[i * G : (i + 1) * G, j * G : (j + 1) * G] = high
            w[i * G : (i + 1) * G, n + j * G : n + (j + 1) * G] = (
                piece - high.astype(jnp.float32)
            ).astype(jnp.bfloat16)

    def window_granule(h, j):
        return h * 8 + 2 * lax.rem(x + j // 2, NX) + lax.rem(j + y, 2)

    def granule_of(ref, p):
        a = tab[0, p]
        piece = ref[a]
        return piece * jnp.full(piece.shape, live[0, p]).astype(piece.dtype)

    def solve_back(h):
        def body(pair, _):
            pieces = [granule_of(cb, window_granule(h, 2 * pair + i)) for i in (0, 1)]
            both = jnp.concatenate(pieces, axis=1)
            twice = jnp.concatenate([both, both], axis=0)
            solved = lax.dot_general(
                twice, w[...], (((0,), (1,)), ((), ())), preferred_element_type=jnp.float32
            ).astype(jnp.bfloat16)
            bt[pl.ds(h * 8 + 2 * pair, 2)] = solved.reshape(2, 2, 64, n)
            return 0

        lax.fori_loop(0, 4, body, 0)

    def solve_in(half):
        def body(pair, _):
            p = half * 8 + 2 * pair
            both = jnp.concatenate([granule_of(ci, p), granule_of(ci, p + 1)], axis=1)
            twice = jnp.concatenate([both, both], axis=0)
            solved = jnp.dot(w[...], twice, preferred_element_type=jnp.float32)
            in_o[:, pl.ds(pl.multiple_of(p * G, 2 * G), 2 * G)] = solved.astype(jnp.bfloat16)
            return 0

        lax.fori_loop(0, 4, body, 0)

    wait_for(loads[1])
    solve_back(1)
    swaps["back1"].start()
    wait_for(loads[2])
    solve_in(1)
    swaps["in1"].start()
    solve_in(0)
    swaps["in0"].start()

    def product(block):
        h, half = block // 2, block % 2
        lhs = jnp.concatenate(
            [bt[pl.ds(h * 8, 8), k].reshape(512, n), bp[pl.ds(h * 8, 8)].reshape(512, n)], axis=1
        )

        def body(pair, _):
            p = half * 8 + 2 * pair
            at = pl.ds(pl.multiple_of(p * G, 2 * G), 2 * G)
            rhs = jnp.concatenate([in_o[:, at], in_p[:, at]], axis=0)
            made = jnp.dot(lhs, rhs, preferred_element_type=jnp.float32)
            for j in range(8):
                g = window_granule(h, j)
                for i in (0, 1):
                    total = -made[j * 64 : (j + 1) * 64, i * G : (i + 1) * G]
                    for ref, which in ((ibo, 0), (ibp, 1)):
                        at_row, at_col = tab[which, g], tab[which, p + i]
                        both = live[which, g] * live[which, p + i]
                        tile = ref[at_col, at_row]
                        total = total + both * tile.astype(jnp.float32)
                    acc[block, j, 2 * pair + i] = total
            return 0

        lax.fori_loop(0, 4, body, 0)

    def copy_of(block, name, tiles, to):
        u = UNIT[block, name]
        size = pl.ds(0, HEAD + 64 * tiles)
        return pltpu.make_async_remote_copy(
            src_ref=sendb.at[u, size], dst_ref=recvb.at[u, size],
            send_sem=send_sem.at[u], recv_sem=recv_sem.at[u],
            device_id=to, device_id_type=MESH,
        )

    copies = []

    def send(block, name, slots, first, last, to):
        u = UNIT[block, name]
        wide = last - first
        most = jnp.full((HEAD, G), 1e-30, jnp.float32)
        for j in slots:
            seen = jnp.abs(acc[block, j, first:last]).reshape(wide * 4, HEAD, G)
            most = jnp.maximum(most, jnp.max(seen, axis=0))
        power = jnp.ceil(jnp.log2(most) + 0.015)
        scale = jnp.exp2(15.0 - power)
        sendb[u, 0:HEAD] = power.astype(jnp.int32).astype(jnp.int16)
        at = HEAD
        for j in slots:
            codes = acc[block, j, first:last].reshape(wide * 4, HEAD, G) * scale[None]
            codes = jnp.round(codes).astype(jnp.int32).astype(jnp.int16)
            sendb[u, at : at + 64 * wide] = codes.reshape(64 * wide, G)
            at += 64 * wide
        copy = copy_of(block, name, len(slots) * wide, to)
        copy.start()
        copies.append(copy)

    def take(block, name, slots, first, last, to, onto=None):
        u = UNIT[block, name]
        wide = last - first
        copy_of(block, name, len(slots) * wide, to).wait_recv()
        scale = jnp.exp2(recvb[u, 0:HEAD].astype(jnp.float32) - 15.0)
        at = HEAD
        onto = block if onto is None else onto
        for j in slots:
            got = recvb[u, at : at + 64 * wide].astype(jnp.float32).reshape(wide * 4, HEAD, G)
            got = (got * scale[None]).reshape(wide, 64, G)
            acc[onto, j, first:last] = acc[onto, j, first:last] + got
            at += 64 * wide

    def b_first(block):
        send(block, "b1p", (4, 5), 0, 4, plus)
        send(block, "b1m", (4, 5), 4, 8, minus)
        send(block, "b2op", (2, 3), 4, 8, plus)
        send(block, "b2om", (6, 7), 0, 4, minus)

    def b_second(block):
        take(block, "b1p", (2, 3), 0, 4, plus)
        send(block, "b2sp", (2, 3), 0, 4, plus)
        take(block, "b1m", (6, 7), 4, 8, minus)
        send(block, "b2sm", (6, 7), 4, 8, minus)

    def b_third(block):
        take(block, "b2op", (0, 1), 4, 8, plus)
        take(block, "b2om", (0, 1), 0, 4, minus)
        take(block, "b2sp", (0, 1), 0, 4, plus)
        take(block, "b2sm", (0, 1), 4, 8, minus)
        send(block, "b3", (1,), 0, 8, over)

    def b_last(block):
        take(block, "b3", (0,), 0, 8, over)

    def a_first(block):
        for d in (2, 1, 3, 0):
            send(block, f"a1_{d}", (2 * d + 1,), 0, 8, over)

    def a_second(block):
        take(block, "a1_2", (4,), 0, 8, over)
        send(block, "a2p", (4,), 0, 4, plus)
        send(block, "a2m", (4,), 4, 8, minus)
        take(block, "a1_1", (2,), 0, 8, over)
        send(block, "a3op", (2,), 4, 8, plus)
        take(block, "a1_3", (6,), 0, 8, over)
        send(block, "a3om", (6,), 0, 4, minus)

    def a_third(block):
        take(block, "a2p", (2,), 0, 4, plus)
        send(block, "a3sp", (2,), 0, 4, plus)
        take(block, "a2m", (6,), 4, 8, minus)
        send(block, "a3sm", (6,), 4, 8, minus)
        take(block, "a1_0", (0,), 0, 8, over)

    def a_last(block):
        take(block, "a3op", (0,), 4, 8, plus)
        take(block, "a3om", (0,), 0, 4, minus)
        take(block, "a3sp", (0,), 0, 4, plus)
        take(block, "a3sm", (0,), 4, 8, minus)

    def emit(block):
        for q in range(8):
            out[block, :, q * G : (q + 1) * G] = acc[block, 0, q]

    wait_for(loads[3])
    for q in range(16):
        swaps[q].wait_recv()
    swaps["back1"].wait_recv()
    swaps["in1"].wait_recv()
    product(3)
    b_first(3)
    swaps["in0"].wait_recv()
    product(2)
    a_first(2)
    solve_back(0)
    swaps["back0"].start()
    b_second(3)
    swaps["back0"].wait_recv()
    product(1)
    b_first(1)
    b_third(3)
    product(0)
    a_first(0)
    b_second(1)
    b_last(3)
    send(3, "carry", (0,), 0, 8, after)
    a_second(2)
    b_third(1)
    a_third(2)
    a_second(0)
    a_last(2)
    emit(2)
    a_third(0)
    b_last(1)
    emit(1)
    take(3, "carry", (0,), 0, 8, after, onto=0)
    a_last(0)
    emit(0)

    for copy in swaps.values():
        copy.wait_send()
    for copy in copies:
        copy.wait_send()


def tables(gran_count, gran_index):
    row = lax.axis_index("row")
    chip = lax.axis_index((X, Y))
    k = lax.axis_index(CORE)
    counts = lax.dynamic_slice(gran_count, (row, 2 * chip, 0), (1, 2, 1))[0]
    index = lax.dynamic_slice(gran_index, (row, 2 * chip, 0, 0), (1, 2, 1, gran_index.shape[-1]))[0, :, 0]
    slots = jnp.arange(index.shape[1], dtype=jnp.int32)
    place = jnp.sum(jnp.where(index[:, :, None] == slots[None, None, :], slots[None, :, None], 0), axis=1)
    live = (place < counts).astype(jnp.float32)
    place = jnp.where(k == 0, place, place[::-1])
    live = jnp.where(k == 0, live, live[::-1])
    return place, live


def on_device(interior_factor, coupling_in, coupling_back, interface_block, gran_count, gran_index):
    factor = interior_factor[0, 0, 0]
    inner = coupling_in[0, 0, 0]
    back = coupling_back[0, 0, 0]
    n, width = inner.shape
    own = interface_block[0, 0, 0].reshape(16, 2, 64, width)
    units = len(UNIT)
    size = HEAD + 64 * 8
    hbm = pl.BlockSpec(memory_space=pl.ANY)
    out = pl.pallas_call(
        kernel,
        out_shape=jax.ShapeDtypeStruct((3, 64, width // 2), jnp.float32),
        in_specs=[pl.BlockSpec(memory_space=pltpu.SMEM)] * 2 + [hbm, hbm, hbm, hbm],
        out_specs=pl.BlockSpec(memory_space=pltpu.VMEM),
        scratch_shapes=[
            pltpu.VMEM((n, n), jnp.float32),
            pltpu.VMEM((16, n, G), jnp.bfloat16),
            pltpu.VMEM((16, n, G), jnp.bfloat16),
            pltpu.VMEM((16, 16, 64, G), jnp.bfloat16),
            pltpu.VMEM((16, 16, 64, G), jnp.bfloat16),
            pltpu.VMEM((n, 2 * n), jnp.bfloat16),
            pltpu.VMEM((n, width), jnp.bfloat16),
            pltpu.VMEM((n, width), jnp.bfloat16),
            pltpu.VMEM((16, 2, 64, n), jnp.bfloat16),
            pltpu.VMEM((16, 64, n), jnp.bfloat16),
            pltpu.VMEM((4, 8, 8, 64, G), jnp.float32),
            pltpu.VMEM((units, size, G), jnp.int16),
            pltpu.VMEM((units, size, G), jnp.int16),
            pltpu.SemaphoreType.DMA,
            pltpu.SemaphoreType.DMA((3, 16)),
            pltpu.SemaphoreType.DMA((20,)),
            pltpu.SemaphoreType.DMA((20,)),
            pltpu.SemaphoreType.DMA((units,)),
            pltpu.SemaphoreType.DMA((units,)),
        ],
        compiler_params=pltpu.CompilerParams(
            collective_id=0, has_side_effects=True, vmem_limit_bytes=56 * 1024 * 1024
        ),
    )(*tables(gran_count, gran_index), factor, inner, back, own)
    return out[None]


def solution(mesh):
    split = Mesh(mesh.devices.reshape(mesh.shape["row"], 4, 2, 2), ("row", X, Y, CORE))
    spec = P("row", COL, None, None, None)
    return jax.shard_map(
        on_device,
        mesh=split,
        in_specs=(spec, spec, spec, spec, P(), P()),
        out_specs=P("row", None, COL, None),
        check_vma=False,
    )
```

time: 966 us -> 66.7 us (0.07); the launches traced: 956 us -> 66.6 us
  waiting for transfers between devices: 737 us -> 0 us
  other arithmetic: 80.5 us -> 1.37 us
  matrix products: 65.5 us -> 0 us
  Pallas kernels: 0 us -> 62.1 us
  local copies, waits for them, and re-layouts: 55 us -> 3.07 us
  between operations: 16.2 us -> 0.01 us
    reduce_scatter x3 -> x0, waiting for transfers between devices: 728 us -> none  [reduced_to_own(): blocks = lax.psum_scatter(blocks, axes[k], scatter_dimension=0, tiled=True)]
    another operation x10 -> x0, other arithmetic: 67.8 us -> none  [the longest x8 61.2 us: solve_block(): lax.linalg.triangular_solve(factor, piece, left_side=True, lower=True)]
    dot_general x3 -> x0, matrix products: 62.6 us -> none  [the longest x2 59.6 us: place(): jnp.einsum('ap,aibj,bq->piqj', table, blocks, table, precision=lax.Precis...]
    pallas_call x0 -> x1, Pallas kernels: none -> 62.1 us  [on_device(): pl.pallas_call(kernel, out_shape=jax.ShapeDtypeStruct((3, 64, width // 2)...]
    transpose x2 -> x0, local copies, waits for them, and re-layouts: 12.8 us -> none  [the longest x1 6.77 us: place(): jnp.einsum('ap,aibj,bq->piqj', table, blocks, table, precision=lax.Precis...]
    unnamed x8 -> x3, local copies, waits for them, and re-layouts: 14.8 us -> 2.25 us
    another operation x22 -> x0, local copies, waits for them, and re-layouts: 12 us -> none  [the longest x20 11.7 us: solve_block(): lax.linalg.triangular_solve(factor, piece, left_side=True, lower=True)]
  transfers between devices with their start and end apart: 4 -> 0, of which waited for: 4 -> 0; matrix products, arithmetic and copies ran while one was open for 0% -> 0% of each run, Pallas kernels for 0% -> 0%
where the time goes in v1:
time: 66.7 us; the launch traced here: 66.6 us
  Pallas kernels  62.1 us (93%)
  local copies, waits for them, and re-layouts  3.07 us (5%)
  other arithmetic  1.37 us (2%)
    pallas_call x1, Pallas kernels, on_device(): pl.pallas_call(kernel, out_shape=jax.ShapeDtypeStruct((3, 64, width // 2)...  62.1 us
    unnamed x3, local copies, waits for them, and re-layouts  2.25 us

profile of v1, /device:TPU:1, one launch (start us, length us, event | category | flops | bytes accessed | tf_op | source)
XLA Modules:
  0.0 66.6 jit_solution(1601112834980891924)
XLA Ops:
  0.0 0.0 copy-start
  0.0 0.8 %dynamic-slice_bitcast_fusion = s32[2]{0:T(128)S(1)} fusion(s32[16,16,1]{1,2,0:T(1,128)} %param.10, s32[]{:T(128)S(6)} %select_n.27, s32[]{:T(128)S(6)} %select_n.28), kind=kLoop, calls=%fused_computation.5 | loop fusion | bytes 24 | tf_op jit(solution)/shard_map/lt | solution.py:359
  0.8 0.2 copy-done
  0.9 0.1 select_reduce_fusion
  1.0 0.1 compare_convert_fusion
  1.1 0.6 broadcast_select_fusion.live
  1.8 0.6 broadcast_select_fusion.1.tab
  2.4 62.1 %shard_map.64 = f32[3,64,1024]{2,1,0:T(8,128)} custom-call(s32[2,16]{1,0:T(2,128)} %broadcast_select_fusion.1.tab, f32[2,16]{1,0:T(2,128)} %broadcast_select_fusion.live, f32[384,384]{1,0:T(8,128)} %bitcast.12, bf16[384,2048]{1,0:T(8,128)(2,1)} %bitcast.10, bf16[384,2048]{1,0:T(8,128)(2,1)} %bitcast.11, bf16[16,2,64,2048]{3,2,1,0:T(8,128)(2,1)} %bitcast.8), custom_call_target="tpu_custom_call" | custom-call | tf_op jit(solution)/shard_map/pallas_call | solution.py:374
  64.5 2.1 %copy.8 = f32[1,3,64,1024]{3,2,1,0:T(8,128)} copy(f32[1,3,64,1024]{3,2,1,0:T(8,128)} %bitcast.9) | data formatting | bytes 1572864
  (3 shorter events, 0.1 us)
Async XLA Ops:
  0.0 0.9 %copy-start = (s32[16,16,1,16]{3,2,1,0:T(1,128)S(1)}, s32[16,16,1,16]{3,2,1,0:T(1,128)}, u32[]{:S(2)}) copy-start(s32[16,16,1,16]{3,2,1,0:T(1,128)} %param.11) | copy-start | bytes 49156

commit v2 on v1

v2 whole, which is shorter than its diff:
```python
import functools

import jax
import jax.numpy as jnp
from jax import lax
from jax.experimental import pallas as pl
from jax.experimental.pallas import tpu as pltpu
from jax.sharding import Mesh
from jax.sharding import PartitionSpec as P

MESH = pl.DeviceIdType.MESH
X, Y, CORE = "col_0", "col_1", "col_2"
COL = (X, Y, CORE)
NX = 4
G = 128
HEAD = 16
HIGHEST = lax.Precision.HIGHEST

Y_FIRST = 7
B_UNITS = ["b1p", "b1m", "b2op", "b2om", "b2sp", "b2sm", "b3"]
A_UNITS = ["a1_2", "a1_1", "a1_3", "a1_0", "a2p", "a2m", "a3op", "a3om", "a3sp", "a3sm"]


def unit_numbers():
    names = [(h, u) for h in (1, 0) for u in B_UNITS + A_UNITS] + [(1, "carry")]
    return {name: i for i, name in enumerate(names)}


UNIT = unit_numbers()


def mm(a, b):
    return jnp.dot(a, b, precision=HIGHEST, preferred_element_type=jnp.float32)


def inverses_of_blocks(blocks):
    n = blocks[0].shape[0]
    row = lax.broadcasted_iota(jnp.int32, (n, n), 0)
    col = lax.broadcasted_iota(jnp.int32, (n, n), 1)

    def below(shift):
        upper, lower = row >> shift, col >> shift
        return ((upper & 1) == 1) & (upper == lower + 1)

    found = []
    for block in blocks:
        diagonal = jnp.where(row == col, block, 0.0)
        down = 1.0 / jnp.sum(diagonal, axis=1, keepdims=True)
        across = 1.0 / jnp.sum(diagonal, axis=0, keepdims=True)
        under = jnp.where(below(0), block, 0.0)
        found.append(jnp.where(row == col, down, 0.0) - under * down * across)
    for shift in range(1, 7):
        mask = below(shift)
        lines = [mm(f, jnp.where(mask, block, 0.0)) for f, block in zip(found, blocks)]
        found = [f - mm(line, f) for f, line in zip(found, lines)]
    return found


def kernel(
    count_hbm, index_hbm, factor_hbm, in_hbm, back_hbm, own_hbm, out,
    counts, index, tab, live, factor, ci, cb, ibo, ibs, ibp, w, in_o, in_p, bt, bp, acc, sendb, recvb,
    factor_sem, load_sem, swap_send, swap_recv, send_sem, recv_sem,
):
    row = lax.axis_index("row")
    rows = lax.axis_size("row")
    x = lax.axis_index(X)
    y = lax.axis_index(Y)
    k = lax.axis_index(CORE)
    plus = {X: lax.rem(x + 1, NX)}
    minus = {X: lax.rem(x + NX - 1, NX)}
    over = {Y: 1 - y}
    mate = {CORE: 1 - k}
    after = {"row": lax.rem(row + 1, rows)}
    before = {"row": lax.rem(row + rows - 1, rows)}

    barrier = pltpu.get_barrier_semaphore()
    for to in (mate, plus, minus, over, after, before):
        pl.semaphore_signal(barrier, inc=1, device_id=to, device_id_type=MESH)

    def load_columns(src, dst, q, which):
        return pltpu.make_async_copy(
            src.at[:, pl.ds(q * G, G)], dst.at[q], load_sem.at[which, q]
        )

    loads = [
        [pltpu.make_async_copy(factor_hbm, factor, factor_sem)],
        [load_columns(back_hbm, cb, q, 0) for q in range(16)],
        [load_columns(in_hbm, ci, q, 1) for q in range(16)],
        [
            pltpu.make_async_copy(
                own_hbm.at[:, :, :, pl.ds(q * G, G)], ibo.at[q], load_sem.at[2, q]
            )
            for q in range(16)
        ],
    ]
    mine = 4 * x + 2 * y + k
    loads[0] += [
        pltpu.make_async_copy(count_hbm.at[row], counts, load_sem.at[3, 0]),
        pltpu.make_async_copy(index_hbm.at[row, mine], index, load_sem.at[3, 1]),
    ]
    def start(load):
        for copy in load:
            copy.start()

    def wait_for(load):
        for copy in load:
            copy.wait()

    start(loads[0])

    def swap(src, dst, n):
        return pltpu.make_async_remote_copy(
            src_ref=src, dst_ref=dst, send_sem=swap_send.at[n], recv_sem=swap_recv.at[n],
            device_id=mate, device_id_type=MESH,
        )

    swaps = {
        "back1": swap(bt.at[pl.ds(8, 8), 1 - k], bp.at[pl.ds(8, 8)], 4),
        "back0": swap(bt.at[pl.ds(0, 8), 1 - k], bp.at[pl.ds(0, 8)], 5),
        "in1": swap(in_o.at[:, pl.ds(1024, 1024)], in_p.at[:, pl.ds(1024, 1024)], 6),
        "in0": swap(in_o.at[:, pl.ds(0, 1024)], in_p.at[:, pl.ds(0, 1024)], 7),
    }
    for block in range(4):
        swaps[block] = swap(ibs.at[block], ibp.at[block], block)

    wait_for(loads[0])
    for load in (loads[3], loads[1], loads[2]):
        start(load)
    n = factor.shape[0]
    at = [index[0, a] for a in range(16)]
    count = counts[mine]
    for p in range(16):
        place = jnp.int32(0)
        for a in range(1, 16):
            place = place + jnp.where(at[a] == p, a, 0)
        tab[0, p] = place & 15
        live[0, p] = jnp.where(place < count, 1.0, 0.0)

    def part(i, j):
        return factor[i * G : (i + 1) * G, j * G : (j + 1) * G]

    x0, x1, x2 = inverses_of_blocks([part(i, i) for i in range(3)])
    x10 = -mm(mm(x1, part(1, 0)), x0)
    t0 = mm(x2, part(2, 0))
    t1 = mm(x2, part(2, 1))
    x20 = -(mm(t0, x0) + mm(t1, x10))
    x21 = -mm(t1, x1)
    zero = jnp.zeros((G, G), jnp.float32)
    for i, line in enumerate(((x0, zero, zero), (x10, x1, zero), (x20, x21, x2))):
        for j, piece in enumerate(line):
            high = piece.astype(jnp.bfloat16)
            w[i * G : (i + 1) * G, j * G : (j + 1) * G] = high
            w[i * G : (i + 1) * G, n + j * G : n + (j + 1) * G] = (
                piece - high.astype(jnp.float32)
            ).astype(jnp.bfloat16)

    def window_granule(h, j):
        return h * 8 + 2 * lax.rem(x + j // 2, NX) + lax.rem(j + y, 2)

    def granule_of(ref, p):
        a = tab[0, p]
        piece = ref[a]
        return piece * jnp.full(piece.shape, live[0, p]).astype(piece.dtype)

    def solve_back(h):
        def body(pair, _):
            pieces = [granule_of(cb, window_granule(h, 2 * pair + i)) for i in (0, 1)]
            both = jnp.concatenate(pieces, axis=1)
            twice = jnp.concatenate([both, both], axis=0)
            solved = lax.dot_general(
                twice, w[...], (((0,), (1,)), ((), ())), preferred_element_type=jnp.float32
            ).astype(jnp.bfloat16)
            bt[pl.ds(h * 8 + 2 * pair, 2)] = solved.reshape(2, 2, 64, n)
            return 0

        lax.fori_loop(0, 4, body, 0)

    def solve_in(half):
        def body(pair, _):
            p = half * 8 + 2 * pair
            both = jnp.concatenate([granule_of(ci, p), granule_of(ci, p + 1)], axis=1)
            twice = jnp.concatenate([both, both], axis=0)
            solved = jnp.dot(w[...], twice, preferred_element_type=jnp.float32)
            in_o[:, pl.ds(pl.multiple_of(p * G, 2 * G), 2 * G)] = solved.astype(jnp.bfloat16)
            return 0

        lax.fori_loop(0, 4, body, 0)

    def gather(block):
        h, half = block // 2, block % 2

        def body(j, _):
            g = window_granule(h, j)
            for q in range(8):
                p = half * 8 + q
                tile = ibo[tab[0, p], tab[0, g], 1 - k]
                keep = jnp.full(tile.shape, live[0, g] * live[0, p]).astype(tile.dtype)
                ibs[block, j, q] = tile * keep
            return 0

        lax.fori_loop(0, 8, body, 0)
        swaps[block].start()

    wait_for(loads[3])
    pl.semaphore_wait(barrier, 6)
    gather(2)
    wait_for(loads[1])
    solve_back(1)
    swaps["back1"].start()
    wait_for(loads[2])
    solve_in(0)
    swaps["in0"].start()
    gather(3)
    solve_in(1)
    swaps["in1"].start()

    def product(block):
        h, half = block // 2, block % 2
        lhs = jnp.concatenate(
            [bt[pl.ds(h * 8, 8), k].reshape(512, n), bp[pl.ds(h * 8, 8)].reshape(512, n)], axis=1
        )

        def body(pair, _):
            p = half * 8 + 2 * pair
            at = pl.ds(pl.multiple_of(p * G, 2 * G), 2 * G)
            rhs = jnp.concatenate([in_o[:, at], in_p[:, at]], axis=0)
            made = jnp.dot(lhs, rhs, preferred_element_type=jnp.float32)
            for j in range(8):
                g = window_granule(h, j)
                for i in (0, 1):
                    total = -made[j * 64 : (j + 1) * 64, i * G : (i + 1) * G]
                    tile = ibo[tab[0, p + i], tab[0, g], k].astype(jnp.float32)
                    total = total + tile * (live[0, g] * live[0, p + i])
                    total = total + ibp[block, j, 2 * pair + i].astype(jnp.float32)
                    acc[h, j, p + i] = total
            return 0

        lax.fori_loop(0, 4, body, 0)

    def copy_of(block, name, tiles, to):
        u = UNIT[block, name]
        size = pl.ds(0, HEAD + 64 * tiles)
        return pltpu.make_async_remote_copy(
            src_ref=sendb.at[u, size], dst_ref=recvb.at[u, size],
            send_sem=send_sem.at[u], recv_sem=recv_sem.at[u],
            device_id=to, device_id_type=MESH,
        )

    copies = []

    def send(block, name, slots, first, last, to):
        u = UNIT[block, name]
        wide = last - first
        most = jnp.full((HEAD, G), 1e-30, jnp.float32)
        for j in slots:
            seen = jnp.abs(acc[block, j, first:last]).reshape(wide * 4, HEAD, G)
            most = jnp.maximum(most, jnp.max(seen, axis=0))
        power = jnp.ceil(jnp.log2(most) + 0.015)
        scale = jnp.exp2(15.0 - power)
        sendb[u, 0:HEAD] = power.astype(jnp.int32).astype(jnp.int16)
        at = HEAD
        for j in slots:
            codes = acc[block, j, first:last].reshape(wide * 4, HEAD, G) * scale[None]
            codes = jnp.round(codes).astype(jnp.int32).astype(jnp.int16)
            sendb[u, at : at + 64 * wide] = codes.reshape(64 * wide, G)
            at += 64 * wide
        copy = copy_of(block, name, len(slots) * wide, to)
        copy.start()
        copies.append(copy)

    def take(block, name, slots, first, last, to, onto=None):
        u = UNIT[block, name]
        wide = last - first
        copy_of(block, name, len(slots) * wide, to).wait_recv()
        scale = jnp.exp2(recvb[u, 0:HEAD].astype(jnp.float32) - 15.0)
        at = HEAD
        h, first, last = (block, first, last) if onto is None else onto
        for j in slots:
            got = recvb[u, at : at + 64 * wide].astype(jnp.float32).reshape(wide * 4, HEAD, G)
            got = (got * scale[None]).reshape(wide, 64, G)
            acc[h, j, first:last] = acc[h, j, first:last] + got
            at += 64 * wide

    a_to, b_to = Y_FIRST, 16
    a_mid = (3, 4)
    b_mid = (12, 11)

    def b_first(h):
        send(h, "b1p", (4, 5), a_to, b_mid[h], plus)
        send(h, "b1m", (4, 5), b_mid[h], b_to, minus)
        send(h, "b2op", (2, 3), b_mid[h], b_to, plus)
        send(h, "b2om", (6, 7), a_to, b_mid[h], minus)

    def b_second(h):
        take(h, "b1p", (2, 3), a_to, b_mid[h], plus)
        send(h, "b2sp", (2, 3), a_to, b_mid[h], plus)
        take(h, "b1m", (6, 7), b_mid[h], b_to, minus)
        send(h, "b2sm", (6, 7), b_mid[h], b_to, minus)

    def b_third(h):
        take(h, "b2op", (0, 1), b_mid[h], b_to, plus)
        take(h, "b2om", (0, 1), a_to, b_mid[h], minus)
        take(h, "b2sp", (0, 1), a_to, b_mid[h], plus)
        take(h, "b2sm", (0, 1), b_mid[h], b_to, minus)
        send(h, "b3", (1,), a_to, b_to, over)

    def b_last(h):
        take(h, "b3", (0,), a_to, b_to, over)

    def a_first(h):
        for d in (2, 1, 3, 0):
            send(h, f"a1_{d}", (2 * d + 1,), 0, a_to, over)

    def a_second(h):
        take(h, "a1_2", (4,), 0, a_to, over)
        send(h, "a2p", (4,), 0, a_mid[h], plus)
        send(h, "a2m", (4,), a_mid[h], a_to, minus)
        take(h, "a1_1", (2,), 0, a_to, over)
        send(h, "a3op", (2,), a_mid[h], a_to, plus)
        take(h, "a1_3", (6,), 0, a_to, over)
        send(h, "a3om", (6,), 0, a_mid[h], minus)

    def a_third(h):
        take(h, "a2p", (2,), 0, a_mid[h], plus)
        send(h, "a3sp", (2,), 0, a_mid[h], plus)
        take(h, "a2m", (6,), a_mid[h], a_to, minus)
        send(h, "a3sm", (6,), a_mid[h], a_to, minus)
        take(h, "a1_0", (0,), 0, a_to, over)

    def a_last(h):
        take(h, "a3op", (0,), a_mid[h], a_to, plus)
        take(h, "a3om", (0,), 0, a_mid[h], minus)
        take(h, "a3sp", (0,), 0, a_mid[h], plus)
        take(h, "a3sm", (0,), a_mid[h], a_to, minus)

    def emit(block):
        h, half = block // 2, block % 2
        for q in range(8):
            out[block, :, q * G : (q + 1) * G] = acc[h, 0, half * 8 + q]

    swaps[2].wait_recv()
    swaps["back1"].wait_recv()
    swaps["in0"].wait_recv()
    product(2)
    a_first(1)
    swaps["in1"].wait_recv()
    swaps[3].wait_recv()
    product(3)
    b_first(1)
    gather(0)
    solve_back(0)
    swaps["back0"].start()
    gather(1)
    b_second(1)
    swaps["back0"].wait_recv()
    swaps[0].wait_recv()
    product(0)
    a_second(1)
    b_third(1)
    a_first(0)
    swaps[1].wait_recv()
    product(1)
    b_first(0)
    a_third(1)
    b_last(1)
    send(1, "carry", (0,), 8, 16, after)
    b_second(0)
    a_second(0)
    a_last(1)
    emit(2)
    b_third(0)
    a_third(0)
    take(1, "carry", (0,), 8, 16, after, onto=(0, 0, 8))
    b_last(0)
    emit(1)
    a_last(0)
    emit(0)

    for copy in swaps.values():
        copy.wait_send()
    for copy in copies:
        copy.wait_send()


def on_device(interior_factor, coupling_in, coupling_back, interface_block, gran_count, gran_index):
    factor = interior_factor[0, 0, 0]
    inner = coupling_in[0, 0, 0]
    back = coupling_back[0, 0, 0]
    n, width = inner.shape
    own = interface_block[0, 0, 0].reshape(16, 2, 64, width)
    units = len(UNIT)
    size = HEAD + 64 * 10
    hbm = pl.BlockSpec(memory_space=pl.ANY)
    out = pl.pallas_call(
        kernel,
        out_shape=pltpu.VMEM((3, 64, width // 2), jnp.float32),
        in_specs=[hbm, hbm, hbm, hbm, hbm, hbm],
        out_specs=pl.BlockSpec(memory_space=pltpu.VMEM),
        scratch_shapes=[
            pltpu.SMEM((16,), jnp.int32),
            pltpu.SMEM((1, 16), jnp.int32),
            pltpu.SMEM((1, 16), jnp.int32),
            pltpu.SMEM((1, 16), jnp.float32),
            pltpu.VMEM((n, n), jnp.float32),
            pltpu.VMEM((16, n, G), jnp.bfloat16),
            pltpu.VMEM((16, n, G), jnp.bfloat16),
            pltpu.VMEM((16, 16, 2, 64, G), jnp.bfloat16),
            pltpu.VMEM((4, 8, 8, 64, G), jnp.bfloat16),
            pltpu.VMEM((4, 8, 8, 64, G), jnp.bfloat16),
            pltpu.VMEM((n, 2 * n), jnp.bfloat16),
            pltpu.VMEM((n, width), jnp.bfloat16),
            pltpu.VMEM((n, width), jnp.bfloat16),
            pltpu.VMEM((16, 2, 64, n), jnp.bfloat16),
            pltpu.VMEM((16, 64, n), jnp.bfloat16),
            pltpu.VMEM((2, 8, 16, 64, G), jnp.float32),
            pltpu.VMEM((units, size, G), jnp.int16),
            pltpu.VMEM((units, size, G), jnp.int16),
            pltpu.SemaphoreType.DMA,
            pltpu.SemaphoreType.DMA((4, 16)),
            pltpu.SemaphoreType.DMA((8,)),
            pltpu.SemaphoreType.DMA((8,)),
            pltpu.SemaphoreType.DMA((units,)),
            pltpu.SemaphoreType.DMA((units,)),
        ],
        compiler_params=pltpu.CompilerParams(
            collective_id=0, has_side_effects=True, vmem_limit_bytes=56 * 1024 * 1024
        ),
    )(gran_count[:, :, 0], gran_index, factor, inner, back, own)
    return out[None]


def solution(mesh):
    split = Mesh(mesh.devices.reshape(mesh.shape["row"], 4, 2, 2), ("row", X, Y, CORE))
    spec = P("row", COL, None, None, None)
    return jax.shard_map(
        on_device,
        mesh=split,
        in_specs=(spec, spec, spec, spec, P(), P()),
        out_specs=P("row", None, COL, None),
        check_vma=False,
    )
```

time: 66.7 us -> 55.8 us (0.84)
  Pallas kernels: 62.1 us -> 54.8 us
  local copies, waits for them, and re-layouts: 3.07 us -> 0.88 us
  other arithmetic: 1.37 us -> 0 us
    pallas_call x1, Pallas kernels: 62.1 us -> 54.8 us  [on_device(): pl.pallas_call(kernel, out_shape=pltpu.VMEM((3, 64, width // 2), jnp.floa...]
    unnamed x3 -> x1, local copies, waits for them, and re-layouts: 2.25 us -> 0.88 us
    select_n x2 -> x0, other arithmetic: 1.21 us -> none  [the longest x1 0.64 us: tables(): live = jnp.where(k == 0, live, live[::-1])]
    lt x1 -> x0, local copies, waits for them, and re-layouts: 0.76 us -> none  [tables(): live = (place < counts).astype(jnp.float32)]
where the time goes in v2:
time: 55.8 us; the launch traced here: 55.7 us
  Pallas kernels  54.8 us (98%)
  local copies, waits for them, and re-layouts  0.88 us (2%)
    pallas_call x1, Pallas kernels, on_device(): pl.pallas_call(kernel, out_shape=pltpu.VMEM((3, 64, width // 2), jnp.floa...  54.8 us

profile of v2, /device:TPU:1, one launch (start us, length us, event | category | flops | bytes accessed | tf_op | source)
XLA Modules:
  0.0 55.7 jit_solution(8516908614693990073)
XLA Ops:
  0.0 54.8 %shard_map.64 = f32[3,64,1024]{2,1,0:T(8,128)S(1)} custom-call(s32[16,16]{1,0:T(8,128)} %bitcast.11, s32[16,16,1,16]{3,2,1,0:T(1,128)} %index_hbm.1, f32[384,384]{1,0:T(8,128)} %bitcast.10, bf16[384,2048]{1,0:T(8,128)(2,1)} %bitcast.8, bf16[384,2048]{1,0:T(8,128)(2,1)} %bitcast.9, bf16[16,2,64,2048]{3,2,1,0:T(8,128)(2,1)} %bitcast.7), custom_call_target="tpu_custom_call" | custom-call | tf_op jit(solution)/shard_map/pallas_call | solution.py:394
  54.8 0.9 %copy.8 = f32[1,3,64,1024]{3,2,1,0:T(8,128)} copy(f32[1,3,64,1024]{3,2,1,0:T(8,128)S(1)} %bitcast.6) | data formatting | bytes 1572864

commit v3 on v2

--- a/solution.py
+++ b/solution.py
@@ -173,7 +173,7 @@
             bt[pl.ds(h * 8 + 2 * pair, 2)] = solved.reshape(2, 2, 64, n)
             return 0
 
-        lax.fori_loop(0, 4, body, 0)
+        lax.fori_loop(0, 4, body, 0, unroll=True)
 
     def solve_in(half):
         def body(pair, _):
@@ -184,7 +184,7 @@
             in_o[:, pl.ds(pl.multiple_of(p * G, 2 * G), 2 * G)] = solved.astype(jnp.bfloat16)
             return 0
 
-        lax.fori_loop(0, 4, body, 0)
+        lax.fori_loop(0, 4, body, 0, unroll=True)
 
     def gather(block):
         h, half = block // 2, block % 2
@@ -198,19 +198,20 @@
                 ibs[block, j, q] = tile * keep
             return 0
 
-        lax.fori_loop(0, 8, body, 0)
-        swaps[block].start()
+        lax.fori_loop(0, 8, body, 0, unroll=2)
 
     wait_for(loads[3])
-    pl.semaphore_wait(barrier, 6)
     gather(2)
     wait_for(loads[1])
     solve_back(1)
+    pl.semaphore_wait(barrier, 6)
+    swaps[2].start()
     swaps["back1"].start()
     wait_for(loads[2])
     solve_in(0)
     swaps["in0"].start()
     gather(3)
+    swaps[3].start()
     solve_in(1)
     swaps["in1"].start()
 
@@ -235,7 +236,7 @@
                     acc[h, j, p + i] = total
             return 0
 
-        lax.fori_loop(0, 4, body, 0)
+        lax.fori_loop(0, 4, body, 0, unroll=True)
 
     def copy_of(block, name, tiles, to):
         u = UNIT[block, name]
@@ -307,8 +308,8 @@
     def b_last(h):
         take(h, "b3", (0,), a_to, b_to, over)
 
-    def a_first(h):
-        for d in (2, 1, 3, 0):
+    def a_first(h, order=(2, 1, 3, 0)):
+        for d in order:
             send(h, f"a1_{d}", (2 * d + 1,), 0, a_to, over)
 
     def a_second(h):
@@ -348,32 +349,35 @@
     product(3)
     b_first(1)
     gather(0)
+    swaps[0].start()
     solve_back(0)
     swaps["back0"].start()
     gather(1)
+    swaps[1].start()
     b_second(1)
     swaps["back0"].wait_recv()
     swaps[0].wait_recv()
     product(0)
+    a_first(0, (2,))
     a_second(1)
     b_third(1)
-    a_first(0)
+    a_first(0, (1, 3, 0))
     swaps[1].wait_recv()
     product(1)
     b_first(0)
-    a_third(1)
     b_last(1)
     send(1, "carry", (0,), 8, 16, after)
+    a_third(1)
     b_second(0)
     a_second(0)
     a_last(1)
     emit(2)
     b_third(0)
     a_third(0)
-    take(1, "carry", (0,), 8, 16, after, onto=(0, 0, 8))
     b_last(0)
     emit(1)
     a_last(0)
+    take(1, "carry", (0,), 8, 16, after, onto=(0, 0, 8))
     emit(0)
 
     for copy in swaps.values():

time: 55.8 us -> 52.3 us (0.937)
  Pallas kernels: 54.8 us -> 51.3 us
    pallas_call x1, Pallas kernels: 54.8 us -> 51.3 us  [on_device(): pl.pallas_call(kernel, out_shape=pltpu.VMEM((3, 64, width // 2), jnp.floa...]
where the time goes in v3:
time: 52.3 us; the launch traced here: 52.2 us
  Pallas kernels  51.3 us (98%)
  local copies, waits for them, and re-layouts  0.88 us (2%)
    pallas_call x1, Pallas kernels, on_device(): pl.pallas_call(kernel, out_shape=pltpu.VMEM((3, 64, width // 2), jnp.floa...  51.3 us

profile of v3, /device:TPU:1, one launch (start us, length us, event | category | flops | bytes accessed | tf_op | source)
XLA Modules:
  0.0 52.2 jit_solution(4285091317524702491)
XLA Ops:
  0.0 51.3 %shard_map.64 = f32[3,64,1024]{2,1,0:T(8,128)S(1)} custom-call(s32[16,16]{1,0:T(8,128)} %bitcast.11, s32[16,16,1,16]{3,2,1,0:T(1,128)} %index_hbm.1, f32[384,384]{1,0:T(8,128)} %bitcast.10, bf16[384,2048]{1,0:T(8,128)(2,1)} %bitcast.8, bf16[384,2048]{1,0:T(8,128)(2,1)} %bitcast.9, bf16[16,2,64,2048]{3,2,1,0:T(8,128)(2,1)} %bitcast.7), custom_call_target="tpu_custom_call" | custom-call | tf_op jit(solution)/shard_map/pallas_call | solution.py:398
  51.3 0.9 %copy.8 = f32[1,3,64,1024]{3,2,1,0:T(8,128)} copy(f32[1,3,64,1024]{3,2,1,0:T(8,128)S(1)} %bitcast.6) | data formatting | bytes 1572864

commit v4 on v3

--- a/solution.py
+++ b/solution.py
@@ -215,10 +215,11 @@
     solve_in(1)
     swaps["in1"].start()
 
-    def product(block):
+    def product(block, part):
         h, half = block // 2, block % 2
+        line = 8 * h + 4 * part
         lhs = jnp.concatenate(
-            [bt[pl.ds(h * 8, 8), k].reshape(512, n), bp[pl.ds(h * 8, 8)].reshape(512, n)], axis=1
+            [bt[pl.ds(line, 4), k].reshape(256, n), bp[pl.ds(line, 4)].reshape(256, n)], axis=1
         )
 
         def body(pair, _):
@@ -226,10 +227,11 @@
             at = pl.ds(pl.multiple_of(p * G, 2 * G), 2 * G)
             rhs = jnp.concatenate([in_o[:, at], in_p[:, at]], axis=0)
             made = jnp.dot(lhs, rhs, preferred_element_type=jnp.float32)
-            for j in range(8):
+            for j in range(4 * part, 4 * part + 4):
                 g = window_granule(h, j)
                 for i in (0, 1):
-                    total = -made[j * 64 : (j + 1) * 64, i * G : (i + 1) * G]
+                    at_row = (j - 4 * part) * 64
+                    total = -made[at_row : at_row + 64, i * G : (i + 1) * G]
                     tile = ibo[tab[0, p + i], tab[0, g], k].astype(jnp.float32)
                     total = total + tile * (live[0, g] * live[0, p + i])
                     total = total + ibp[block, j, 2 * pair + i].astype(jnp.float32)
@@ -289,8 +291,10 @@
     def b_first(h):
         send(h, "b1p", (4, 5), a_to, b_mid[h], plus)
         send(h, "b1m", (4, 5), b_mid[h], b_to, minus)
+        send(h, "b2om", (6, 7), a_to, b_mid[h], minus)
+
+    def b_direct(h):
         send(h, "b2op", (2, 3), b_mid[h], b_to, plus)
-        send(h, "b2om", (6, 7), a_to, b_mid[h], minus)
 
     def b_second(h):
         take(h, "b1p", (2, 3), a_to, b_mid[h], plus)
@@ -342,12 +346,16 @@
     swaps[2].wait_recv()
     swaps["back1"].wait_recv()
     swaps["in0"].wait_recv()
-    product(2)
-    a_first(1)
+    product(2, 1)
+    a_first(1, (2, 3))
+    product(2, 0)
+    a_first(1, (1, 0))
     swaps["in1"].wait_recv()
     swaps[3].wait_recv()
-    product(3)
+    product(3, 1)
     b_first(1)
+    product(3, 0)
+    b_direct(1)
     gather(0)
     swaps[0].start()
     solve_back(0)
@@ -357,22 +365,25 @@
     b_second(1)
     swaps["back0"].wait_recv()
     swaps[0].wait_recv()
-    product(0)
+    product(0, 1)
+    product(0, 0)
     a_first(0, (2,))
     a_second(1)
     b_third(1)
     a_first(0, (1, 3, 0))
     swaps[1].wait_recv()
-    product(1)
+    product(1, 1)
     b_first(0)
+    product(1, 0)
+    b_direct(0)
     b_last(1)
     send(1, "carry", (0,), 8, 16, after)
+    b_second(0)
     a_third(1)
-    b_second(0)
     a_second(0)
+    b_third(0)
     a_last(1)
     emit(2)
-    b_third(0)
     a_third(0)
     b_last(0)
     emit(1)

time: 52.3 us -> 51.4 us (0.983)
  Pallas kernels: 51.3 us -> 50.4 us
    pallas_call x1, Pallas kernels: 51.3 us -> 50.4 us  [on_device(): pl.pallas_call(kernel, out_shape=pltpu.VMEM((3, 64, width // 2), jnp.floa...]
where the time goes in v4:
time: 51.4 us; the launch traced here: 51.3 us
  Pallas kernels  50.4 us (98%)
  local copies, waits for them, and re-layouts  0.88 us (2%)
    pallas_call x1, Pallas kernels, on_device(): pl.pallas_call(kernel, out_shape=pltpu.VMEM((3, 64, width // 2), jnp.floa...  50.4 us

profile of v4, /device:TPU:1, one launch (start us, length us, event | category | flops | bytes accessed | tf_op | source)
XLA Modules:
  0.0 51.3 jit_solution(10378552255351007883)
XLA Ops:
  0.0 50.4 %shard_map.64 = f32[3,64,1024]{2,1,0:T(8,128)S(1)} custom-call(s32[16,16]{1,0:T(8,128)} %bitcast.11, s32[16,16,1,16]{3,2,1,0:T(1,128)} %index_hbm.1, f32[384,384]{1,0:T(8,128)} %bitcast.10, bf16[384,2048]{1,0:T(8,128)(2,1)} %bitcast.8, bf16[384,2048]{1,0:T(8,128)(2,1)} %bitcast.9, bf16[16,2,64,2048]{3,2,1,0:T(8,128)(2,1)} %bitcast.7), custom_call_target="tpu_custom_call" | custom-call | tf_op jit(solution)/shard_map/pallas_call | solution.py:409
  50.4 0.9 %copy.8 = f32[1,3,64,1024]{3,2,1,0:T(8,128)} copy(f32[1,3,64,1024]{3,2,1,0:T(8,128)S(1)} %bitcast.6) | data formatting | bytes 1572864
